TPU v7x, 128 devices: a whole 4x4x4 slice. The times are simulated.
128 devices in a mesh: gx: 8 (over x, core), gy: 16 (over y, z).
Axes of the slice: x: 4, y: 4, z: 4, core: 2. Of those that a mesh axis runs over, the one named last changes fastest.
Arguments:
- state: float32 [32, 768, 2048], P('gx', None, 'gy'), may hold values from -6 to 6
- forcing: float32 [32, 768, 2048], P('gx', None, 'gy'), may hold values from -6 to 6
- vertical_mix: float32 [768, 768], replicated, may hold values from -0.21875 to 0.21875
- diffusion: float32 [768], replicated, may hold values from 0.1 to 1
- column_class: int32 [32, 2048], P('gx', 'gy'), may hold values from 0 to 2
- block_regime: int32 [16, 32, 1], P('gy', 'gx'), may hold values from 0 to 7; in each aligned block of 4 rows (0 to 3, 4 to 7, ..., all dimensions but the last counted through in order) no two rows name the same one
- correction_ops: float32 [8, 768, 768], P('gx'), may hold values from -0.21875 to 0.21875
Outputs:
- new_state: float32 [32, 768, 2048], P('gx', None, 'gy')
Inputs may be any that keep to these rules, and one draw needn't show every extreme that they name: `block_regime`: among the blocks of one device (the same first index, 4 consecutive grid rows) no regime appears twice.
All inputs are finite; a program needn't handle non-finite values.
Results may differ from a plain program's by a relative error of at most 0.0002.
Values sent between devices are 32-bit elements; how exact they have to be, the bound alone decides.
No kernel may reach another device: no remote copies, remote signals or barrier semaphores. Data moves between devices by JAX's collectives and lax.ppermute only.
A program may use at most 128 MiB of HBM per device.

v0:
```python
import functools
import jax
import jax.numpy as jnp
from jax import lax
from jax.sharding import Mesh
from jax.sharding import PartitionSpec as P

ITERS = 4
GX_GY = ("gx_0", "gx_1", "gy_0", "gy_1")
GX = ("gx_0", "gx_1")
GY = ("gy_0", "gy_1")


def one_axis_at_a_time(array, axes):
    return functools.reduce(lax.psum, axes, array)


def padded_2(array, sides, width):
    edges = {}
    for axis, dim in sides:
        devices, length = (lax.axis_size(axis), array.shape[dim])
        up = [(i, (i + 1) % devices) for i in range(devices - 1)]
        last = lax.slice_in_dim(array, length - width, length, axis=dim)
        first = lax.slice_in_dim(array, 0, width, axis=dim)
        edges[dim] = (
            lax.ppermute(last, axis, up),
            lax.ppermute(first, axis, [(b, a) for a, b in up]),
        )
    done = []
    for _, dim in sides:
        low, high = edges[dim]
        around = [(width, width) if d in done else (0, 0) for d in range(array.ndim)]
        array = jnp.concatenate([jnp.pad(low, around), array, jnp.pad(high, around)], axis=dim)
        done.append(dim)
    return array


def squares(field):
    return one_axis_at_a_time(jnp.sum(field * field), GX_GY)


def chol_solve(factor, target):
    count = target.shape[0]
    forward = []
    for index in range(count):
        value = target[index]
        for other in range(index):
            value = value - factor[index, other] * forward[other]
        forward.append(value / factor[index, index])
    backward = [None] * count
    for index in range(count - 1, -1, -1):
        value = forward[index]
        for other in range(index + 1, count):
            value = value - factor[other, index] * backward[other]
        backward[index] = value / factor[index, index]
    return jnp.stack(backward)


def local(state, forcing, vertical_mix, diffusion, column_class, block_regime, correction_ops):
    highest = lax.Precision.HIGHEST
    regimes = block_regime[0, :, 0]
    weights = (column_class.astype(jnp.float32) * 0.5)[:, None, :]
    coeff_rows = diffusion[None, :, None]

    def spread(field):
        padded = padded_2(field, ((GX, 0), (GY, 2)), 1)
        centre = padded[1:-1, :, 1:-1]
        lap = (
            4.0 * centre
            - padded[2:, :, 1:-1]
            - padded[:-2, :, 1:-1]
            - padded[1:-1, :, 2:]
            - padded[1:-1, :, :-2]
        )
        mixed = jnp.einsum("pq,xqy->xpy", vertical_mix, field, precision=highest)
        return 2.0 * field + mixed + coeff_rows * lap

    every_op = lax.all_gather(correction_ops, GX, axis=0, tiled=True)
    chosen = every_op[regimes]

    def correct(field):
        return jnp.einsum("bpq,bqc->bpc", chosen, field, precision=highest) * weights

    shade = jnp.tanh(state)
    slope = 1.0 - shade * shade
    residual = forcing - (spread(state) + correct(shade))
    beta = jnp.sqrt(squares(residual) + 1e-12)
    basis = [residual / beta]
    columns = []
    for step in range(ITERS):
        current = basis[-1]
        image = spread(current) + correct(slope * current)
        locals_sum = jnp.stack([jnp.sum(vector * image) for vector in basis])
        coefs = one_axis_at_a_time(locals_sum, GX_GY)
        for index in range(len(basis)):
            image = image - coefs[index] * basis[index]
        length = jnp.sqrt(squares(image) + 1e-12)
        column = jnp.concatenate([coefs, length[None], jnp.zeros((ITERS - step - 1,), jnp.float32)])
        columns.append(column)
        if step + 1 < ITERS:
            basis.append(image / length)
    hess = jnp.stack(columns, axis=1)
    gram = jnp.dot(hess.T, hess, precision=highest)
    target = beta * hess[0]
    factor = jnp.linalg.cholesky(gram)
    solved = chol_solve(factor, target)
    new_state = state
    for index in range(ITERS):
        new_state = new_state + solved[index] * basis[index]
    return new_state


def solution(mesh):
    finer = Mesh(mesh.devices.reshape(4, 2, 4, 4), ("gx_0", "gx_1", "gy_0", "gy_1"))
    in_specs = (
        P(GX, None, GY),
        P(GX, None, GY),
        P(),
        P(),
        P(GX, GY),
        P(GY, GX, None),
        P(GX, None, None),
    )
    out_specs = P(GX, None, GY)
    return jax.shard_map(local, mesh=finer, in_specs=in_specs, out_specs=out_specs, check_vma=False)
```

profile of v0, /device:TPU:34, one launch (start us, length us, event | category | flops | bytes accessed | tf_op | source)
XLA Modules:
  0.0 631.4 jit_solution(1450121057735657620)
XLA Ops:
  27.3 81.3 %all-gather.2.cloned.1.call-done = f32[8,768,768]{2,1,0:T(8,128)} async-done(((f32[1,768,768]{2,1,0:T(8,128)}), f32[8,768,768]{2,1,0:T(8,128)}) %all-gather.2.cloned.1.call-update) | async-done | bytes 18874384 | tf_op jit(solution)/shard_map/all_gather | solution.py:78
  108.7 11.2 %gather_fusion = f32[4,768,768]{2,1,0:T(8,128)} fusion(f32[8,768,768]{2,1,0:T(8,128)} %all-gather.2.cloned.1.call-done, s32[1024]{0:T(1024)S(1)} %pad_clamp_fusion), kind=kCustom, calls=%fused_computation | custom fusion | bytes 18874384 | tf_op jit(solution)/shard_map/gather | solution.py:79
  119.9 13.6 %fusion.74 = f32[4,768,128]{1,2,0:T(8,128)S(1)} fusion(f32[4,768,768]{2,1,0:T(8,128)} %gather_fusion, f32[4,768,128]{1,2,0:T(8,128)} %copy.40), kind=kOutput, calls=%fused_computation.132 | convolution fusion | flops 3623878656 | bytes 12582912 | tf_op jit(solution)/shard_map/bpq,bqc->bpc/dot_general | solution.py:82
  133.7 11.4 %multiply_reduce_fusion.14 = (f32[]{:T(128)}, f32[4,768,128]{1,2,0:T(8,128)}) fusion(f32[4,768,128]{1,2,0:T(8,128)S(1)} %copy-done.16, f32[4,768,128]{1,2,0:T(8,128)S(1)} %fusion.74, f32[4,128]{1,0:T(4,128)S(1)} %convert_multiply_fusion, f32[1,768,128]{1,2,0:T(8,128)} %collective-permute-done, f32[4,768,128]{1,2,0:T(8,128)S(1)} %copy-done.1, ...), kind=kOutput, calls=%fused_computation.131 | convolution fusion | flops 3634888704 | bytes 11039748 | tf_op jit(solution)/shard_map/pq,xqy->xpy/dot_general | solution.py:75
  145.0 8.9 %psum.252 = f32[]{:T(128)} all-reduce(f32[]{:T(128)} %get-tuple-element.61), channel_id=1, replica_groups=mesh['gx_0'=4,'gx_1'=2,'gy_0'=4,'gy_1'=4] {'gx_0'}, use_global_device_ids=true, to_apply=%region_1.2 | all-reduce | flops 1 | bytes 8 | tf_op jit(solution)/shard_map/psum | solution.py:15
  157.2 11.1 %psum.254 = f32[]{:T(128)} all-reduce(f32[]{:T(128)} %psum.253), channel_id=1, replica_groups=mesh['gx_0'=4,'gx_1'=2,'gy_0'=4,'gy_1'=4] {'gy_0'}, use_global_device_ids=true, to_apply=%region_3.4 | all-reduce | flops 1 | bytes 8 | tf_op jit(solution)/shard_map/psum | solution.py:15
  168.3 9.3 %psum.255 = f32[]{:T(128)} all-reduce(f32[]{:T(128)} %psum.254), channel_id=1, replica_groups=mesh['gx_0'=4,'gx_1'=2,'gy_0'=4,'gy_1'=4] {'gy_1'}, use_global_device_ids=true, to_apply=%region_4.5 | all-reduce | flops 1 | bytes 8 | tf_op jit(solution)/shard_map/psum | solution.py:15
  191.5 12.6 %fusion.62 = f32[4,768,128]{1,2,0:T(8,128)S(1)} fusion(f32[4,768,768]{2,1,0:T(8,128)} %gather_fusion, f32[4,768,128]{1,2,0:T(8,128)S(1)} %broadcast_divide_fusion.3, f32[4,768,128]{1,2,0:T(8,128)S(1)} %copy-done.2), kind=kOutput, calls=%fused_computation.128 | convolution fusion | flops 3625058304 | bytes 14155776 | tf_op jit(solution)/shard_map/bpq,bqc->bpc/dot_general | solution.py:82
  204.1 6.6 %multiply_reduce_fusion.13 = (f32[]{:T(128)}, f32[4,768,128]{1,2,0:T(8,128)}) fusion(f32[4,768,128]{1,2,0:T(8,128)S(1)} %broadcast_divide_fusion.3, f32[4,768,128]{1,2,0:T(8,128)S(1)} %fusion.62, f32[4,128]{1,0:T(4,128)S(1)} %convert_multiply_fusion, f32[1,768,128]{1,2,0:T(8,128)S(1)} %collective-permute-done.4, ...), kind=kOutput, calls=%fused_computation.127 | convolution fusion | flops 3634495488 | bytes 7894020 | tf_op jit(solution)/shard_map/pq,xqy->xpy/dot_general | solution.py:75
  210.7 8.0 %psum.256 = f32[1]{0:T(128)} all-reduce(f32[1]{0:T(128)} %bitcast.5), channel_id=1, replica_groups=mesh['gx_0'=4,'gx_1'=2,'gy_0'=4,'gy_1'=4] {'gx_0'}, use_global_device_ids=true, to_apply=%region_6.7 | all-reduce | flops 1 | bytes 8 | tf_op jit(solution)/shard_map/psum | solution.py:15
  221.8 8.4 %psum.258 = f32[1]{0:T(128)} all-reduce(f32[1]{0:T(128)} %psum.257), channel_id=1, replica_groups=mesh['gx_0'=4,'gx_1'=2,'gy_0'=4,'gy_1'=4] {'gy_0'}, use_global_device_ids=true, to_apply=%region_8.9 | all-reduce | flops 1 | bytes 8 | tf_op jit(solution)/shard_map/psum | solution.py:15
  230.2 10.3 %psum.259 = f32[1]{0:T(128)} all-reduce(f32[1]{0:T(128)} %psum.258), channel_id=1, replica_groups=mesh['gx_0'=4,'gx_1'=2,'gy_0'=4,'gy_1'=4] {'gy_1'}, use_global_device_ids=true, to_apply=%region_9.10 | all-reduce | flops 1 | bytes 8 | tf_op jit(solution)/shard_map/psum | solution.py:15
  244.0 10.7 %psum.260 = f32[]{:T(128)} all-reduce(f32[]{:T(128)} %multiply_reduce_fusion.12), channel_id=1, replica_groups=mesh['gx_0'=4,'gx_1'=2,'gy_0'=4,'gy_1'=4] {'gx_0'}, use_global_device_ids=true, to_apply=%region_11.12 | all-reduce | flops 1 | bytes 8 | tf_op jit(solution)/shard_map/psum | solution.py:15
  257.9 9.8 %psum.262 = f32[]{:T(128)} all-reduce(f32[]{:T(128)} %psum.261), channel_id=1, replica_groups=mesh['gx_0'=4,'gx_1'=2,'gy_0'=4,'gy_1'=4] {'gy_0'}, use_global_device_ids=true, to_apply=%region_13.14 | all-reduce | flops 1 | bytes 8 | tf_op jit(solution)/shard_map/psum | solution.py:15
  267.7 11.0 %psum.263 = f32[]{:T(128)} all-reduce(f32[]{:T(128)} %psum.262), channel_id=1, replica_groups=mesh['gx_0'=4,'gx_1'=2,'gy_0'=4,'gy_1'=4] {'gy_1'}, use_global_device_ids=true, to_apply=%region_14.15 | all-reduce | flops 1 | bytes 8 | tf_op jit(solution)/shard_map/psum | solution.py:15
  284.3 3.9 collective-permute-start.11
  290.2 4.2 collective-permute-start.8
  294.4 12.6 %fusion.60 = f32[4,768,128]{1,2,0:T(8,128)S(1)} fusion(f32[4,768,768]{2,1,0:T(8,128)} %gather_fusion, f32[4,768,128]{1,2,0:T(8,128)S(1)} %broadcast_divide_fusion.2, f32[4,768,128]{1,2,0:T(8,128)S(1)} %copy-done.3), kind=kOutput, calls=%fused_computation.123 | convolution fusion | flops 3625058304 | bytes 14155776 | tf_op jit(solution)/shard_map/bpq,bqc->bpc/dot_general | solution.py:82
  307.0 6.7 %multiply_reduce_fusion.11 = (f32[]{:T(128)}, f32[]{:T(128)}, f32[4,768,128]{1,2,0:T(8,128)}) fusion(f32[4,768,128]{1,2,0:T(8,128)S(1)} %copy-done.10, f32[4,768,128]{1,2,0:T(8,128)S(1)} %broadcast_divide_fusion.2, f32[4,768,128]{1,2,0:T(8,128)S(1)} %fusion.60, f32[4,128]{1,0:T(4,128)S(1)} %convert_multiply_fusion, ...), kind=kOutput, calls=%fused_computation.122 | convolution fusion | flops 3635281920 | bytes 9466888 | tf_op jit(solution)/shard_map/pq,xqy->xpy/dot_general | solution.py:75
  315.0 6.5 %psum.264 = f32[2]{0:T(128)S(1)} all-reduce(f32[2]{0:T(128)S(1)} %pad_maximum_fusion.31), channel_id=1, replica_groups=mesh['gx_0'=4,'gx_1'=2,'gy_0'=4,'gy_1'=4] {'gx_0'}, use_global_device_ids=true, to_apply=%region_17.18 | all-reduce | flops 2 | bytes 16 | tf_op jit(solution)/shard_map/psum | solution.py:15
  324.0 7.7 %psum.266 = f32[2]{0:T(128)S(1)} all-reduce(f32[2]{0:T(128)S(1)} %psum.265), channel_id=1, replica_groups=mesh['gx_0'=4,'gx_1'=2,'gy_0'=4,'gy_1'=4] {'gy_0'}, use_global_device_ids=true, to_apply=%region_19.20 | all-reduce | flops 2 | bytes 16 | tf_op jit(solution)/shard_map/psum | solution.py:15
  331.7 9.2 %psum.267 = f32[2]{0:T(128)S(1)} all-reduce(f32[2]{0:T(128)S(1)} %psum.266), channel_id=1, replica_groups=mesh['gx_0'=4,'gx_1'=2,'gy_0'=4,'gy_1'=4] {'gy_1'}, use_global_device_ids=true, to_apply=%region_20.21 | all-reduce | flops 2 | bytes 16 | tf_op jit(solution)/shard_map/psum | solution.py:15
  341.5 5.7 multiply_reduce_fusion.9
  347.2 11.6 %psum.268 = f32[]{:T(128)} all-reduce(f32[]{:T(128)} %get-tuple-element.16), channel_id=1, replica_groups=mesh['gx_0'=4,'gx_1'=2,'gy_0'=4,'gy_1'=4] {'gx_0'}, use_global_device_ids=true, to_apply=%region_22.23 | all-reduce | flops 1 | bytes 8 | tf_op jit(solution)/shard_map/psum | solution.py:15
  362.0 9.9 %psum.270 = f32[]{:T(128)} all-reduce(f32[]{:T(128)} %psum.269), channel_id=1, replica_groups=mesh['gx_0'=4,'gx_1'=2,'gy_0'=4,'gy_1'=4] {'gy_0'}, use_global_device_ids=true, to_apply=%region_24.25 | all-reduce | flops 1 | bytes 8 | tf_op jit(solution)/shard_map/psum | solution.py:15
  371.9 11.6 %psum.271 = f32[]{:T(128)} all-reduce(f32[]{:T(128)} %psum.270), channel_id=1, replica_groups=mesh['gx_0'=4,'gx_1'=2,'gy_0'=4,'gy_1'=4] {'gy_1'}, use_global_device_ids=true, to_apply=%region_25.26 | all-reduce | flops 1 | bytes 8 | tf_op jit(solution)/shard_map/psum | solution.py:15
  388.0 3.9 collective-permute-start.15
  393.9 4.1 collective-permute-start.12
  398.0 12.6 %fusion.58 = f32[4,768,128]{1,2,0:T(8,128)S(1)} fusion(f32[4,768,768]{2,1,0:T(8,128)} %gather_fusion, f32[4,768,128]{1,2,0:T(8,128)S(1)} %broadcast_divide_fusion.1, f32[4,768,128]{1,2,0:T(8,128)S(1)} %copy-done.4), kind=kOutput, calls=%fused_computation.117 | convolution fusion | flops 3625058304 | bytes 14155776 | tf_op jit(solution)/shard_map/bpq,bqc->bpc/dot_general | solution.py:82
  410.6 6.9 %multiply_reduce_fusion.8 = (f32[]{:T(128)}, f32[]{:T(128)}, f32[]{:T(128)}, f32[4,768,128]{1,2,0:T(8,128)}) fusion(f32[4,768,128]{1,2,0:T(8,128)S(1)} %copy-done.11, f32[4,768,128]{1,2,0:T(8,128)S(1)} %broadcast_divide_fusion.1, f32[4,768,128]{1,2,0:T(8,128)S(1)} %copy-done.7, f32[4,768,128]{1,2,0:T(8,128)S(1)} %fusion.58, ...), kind=kOutput, calls=%fused_computation.116 | convolution fusion | flops 3636068352 | bytes 11039756 | tf_op jit(solution)/shard_map/pq,xqy->xpy/dot_general | solution.py:75
  419.5 6.5 %psum.272 = f32[3]{0:T(128)S(1)} all-reduce(f32[3]{0:T(128)S(1)} %pad_maximum_fusion.32), channel_id=1, replica_groups=mesh['gx_0'=4,'gx_1'=2,'gy_0'=4,'gy_1'=4] {'gx_0'}, use_global_device_ids=true, to_apply=%region_29.30 | all-reduce | flops 3 | bytes 24 | tf_op jit(solution)/shard_map/psum | solution.py:15
  428.4 7.7 %psum.274 = f32[3]{0:T(128)S(1)} all-reduce(f32[3]{0:T(128)S(1)} %psum.273), channel_id=1, replica_groups=mesh['gx_0'=4,'gx_1'=2,'gy_0'=4,'gy_1'=4] {'gy_0'}, use_global_device_ids=true, to_apply=%region_31.32 | all-reduce | flops 3 | bytes 24 | tf_op jit(solution)/shard_map/psum | solution.py:15
  436.2 9.2 %psum.275 = f32[3]{0:T(128)S(1)} all-reduce(f32[3]{0:T(128)S(1)} %psum.274), channel_id=1, replica_groups=mesh['gx_0'=4,'gx_1'=2,'gy_0'=4,'gy_1'=4] {'gy_1'}, use_global_device_ids=true, to_apply=%region_32.33 | all-reduce | flops 3 | bytes 24 | tf_op jit(solution)/shard_map/psum | solution.py:15
  446.0 7.1 %multiply_reduce_fusion.5 = (f32[]{:T(128)}, f32[4,768,128]{1,2,0:T(8,128)}) fusion(f32[]{:T(128)} %bitcast.22, f32[4,768,128]{1,2,0:T(8,128)} %copy-done.6, f32[]{:T(128)} %bitcast.21, f32[4,768,128]{1,2,0:T(8,128)} %get-tuple-element.66, f32[]{:T(128)} %bitcast.20, f32[4,768,128]{1,2,0:T(8,128)} %get-tuple-element.17, f32[]{:T(128)} %sqrt.17, ...), kind=kLoop, calls=%fused_computation.112 | loop fusion | flops 3932159 | bytes 7864344 | tf_op jit(solution)/shard_map/reduce_sum | solution.py:39
  453.0 11.6 %psum.276 = f32[]{:T(128)} all-reduce(f32[]{:T(128)} %get-tuple-element.14), channel_id=1, replica_groups=mesh['gx_0'=4,'gx_1'=2,'gy_0'=4,'gy_1'=4] {'gx_0'}, use_global_device_ids=true, to_apply=%region_34.35 | all-reduce | flops 1 | bytes 8 | tf_op jit(solution)/shard_map/psum | solution.py:15
  467.8 9.9 %psum.278 = f32[]{:T(128)} all-reduce(f32[]{:T(128)} %psum.277), channel_id=1, replica_groups=mesh['gx_0'=4,'gx_1'=2,'gy_0'=4,'gy_1'=4] {'gy_0'}, use_global_device_ids=true, to_apply=%region_36.37 | all-reduce | flops 1 | bytes 8 | tf_op jit(solution)/shard_map/psum | solution.py:15
  477.7 11.6 %psum.279 = f32[]{:T(128)} all-reduce(f32[]{:T(128)} %psum.278), channel_id=1, replica_groups=mesh['gx_0'=4,'gx_1'=2,'gy_0'=4,'gy_1'=4] {'gy_1'}, use_global_device_ids=true, to_apply=%region_37.38 | all-reduce | flops 1 | bytes 8 | tf_op jit(solution)/shard_map/psum | solution.py:15
  499.6 4.1 collective-permute-start.16
  503.7 12.6 %fusion.56 = f32[4,768,128]{1,2,0:T(8,128)S(1)} fusion(f32[4,768,768]{2,1,0:T(8,128)} %gather_fusion, f32[4,768,128]{1,2,0:T(8,128)S(1)} %broadcast_divide_fusion, f32[4,768,128]{1,2,0:T(8,128)S(1)} %copy-done.5), kind=kOutput, calls=%fused_computation.110 | convolution fusion | flops 3625058304 | bytes 14155776 | tf_op jit(solution)/shard_map/bpq,bqc->bpc/dot_general | solution.py:82
  516.4 7.0 %multiply_reduce_fusion.4 = (f32[]{:T(128)}, f32[]{:T(128)}, f32[]{:T(128)}, f32[]{:T(128)}, f32[4,768,128]{1,2,0:T(8,128)}) fusion(f32[4,768,128]{1,2,0:T(8,128)S(1)} %copy-done.12, f32[4,768,128]{1,2,0:T(8,128)S(1)} %broadcast_divide_fusion, f32[4,768,128]{1,2,0:T(8,128)S(1)} %copy-done.14, f32[4,768,128]{1,2,0:T(8,128)S(1)} %copy-done.8, ...), kind=kOutput, calls=%fused_computation.109 | convolution fusion | flops 3636854784 | bytes 12612624 | tf_op jit(solution)/shard_map/pq,xqy->xpy/dot_general | solution.py:75
  526.0 6.5 %psum.280 = f32[4]{0:T(128)S(1)} all-reduce(f32[4]{0:T(128)S(1)} %pad_maximum_fusion.33), channel_id=1, replica_groups=mesh['gx_0'=4,'gx_1'=2,'gy_0'=4,'gy_1'=4] {'gx_0'}, use_global_device_ids=true, to_apply=%region_42.43 | all-reduce | flops 4 | bytes 32 | tf_op jit(solution)/shard_map/psum | solution.py:15
  535.0 7.7 %psum.282 = f32[4]{0:T(128)S(1)} all-reduce(f32[4]{0:T(128)S(1)} %psum.281), channel_id=1, replica_groups=mesh['gx_0'=4,'gx_1'=2,'gy_0'=4,'gy_1'=4] {'gy_0'}, use_global_device_ids=true, to_apply=%region_44.45 | all-reduce | flops 4 | bytes 32 | tf_op jit(solution)/shard_map/psum | solution.py:15
  542.7 9.2 %psum.283 = f32[4]{0:T(128)S(1)} all-reduce(f32[4]{0:T(128)S(1)} %psum.282), channel_id=1, replica_groups=mesh['gx_0'=4,'gx_1'=2,'gy_0'=4,'gy_1'=4] {'gy_1'}, use_global_device_ids=true, to_apply=%region_45.46 | all-reduce | flops 4 | bytes 32 | tf_op jit(solution)/shard_map/psum | solution.py:15
  552.6 7.1 %multiply_reduce_fusion = f32[]{:T(128)} fusion(f32[4,768,128]{1,2,0:T(8,128)} %copy-done.6, f32[4,768,128]{1,2,0:T(8,128)} %get-tuple-element.67, f32[]{:T(128)} %bitcast.33, f32[]{:T(128)} %bitcast.32, f32[]{:T(128)} %bitcast.31, f32[]{:T(128)} %bitcast.30, f32[4,768,128]{1,2,0:T(8,128)} %get-tuple-element.15, f32[]{:T(128)} %sqrt.18, ...), kind=kLoop, calls=%fused_computation.105 | loop fusion | flops 5111807 | bytes 7864352 | tf_op jit(solution)/shard_map/reduce_sum | solution.py:39
  559.7 11.6 %psum.284 = f32[]{:T(128)} all-reduce(f32[]{:T(128)} %multiply_reduce_fusion), channel_id=1, replica_groups=mesh['gx_0'=4,'gx_1'=2,'gy_0'=4,'gy_1'=4] {'gx_0'}, use_global_device_ids=true, to_apply=%region_47.48 | all-reduce | flops 1 | bytes 8 | tf_op jit(solution)/shard_map/psum | solution.py:15
  575.1 9.8 %psum.286 = f32[]{:T(128)} all-reduce(f32[]{:T(128)} %psum.285), channel_id=1, replica_groups=mesh['gx_0'=4,'gx_1'=2,'gy_0'=4,'gy_1'=4] {'gy_0'}, use_global_device_ids=true, to_apply=%region_49.50 | all-reduce | flops 1 | bytes 8 | tf_op jit(solution)/shard_map/psum | solution.py:15
  585.0 11.6 %psum.287 = f32[]{:T(128)} all-reduce(f32[]{:T(128)} %psum.286), channel_id=1, replica_groups=mesh['gx_0'=4,'gx_1'=2,'gy_0'=4,'gy_1'=4] {'gy_1'}, use_global_device_ids=true, to_apply=%region_50.51 | all-reduce | flops 1 | bytes 8 | tf_op jit(solution)/shard_map/psum | solution.py:15
  616.1 5.0 multiply_add_fusion
  (130 shorter events, 100.8 us)
Async XLA Ops:
  6.5 127.1 %copy-start = (f32[768,768]{1,0:T(8,128)S(1)}, f32[768,768]{1,0:T(8,128)}, u32[]{:S(2)}) copy-start(f32[768,768]{1,0:T(8,128)} %param.9) | copy-start | bytes 7077892
  6.5 102.1 %all-gather.2.cloned.1.call-start = ((), (), s32[]{:S(2)}) async-start(), calls=%async_computation | async-start | bytes 21233664 | tf_op jit(solution)/shard_map/all_gather | solution.py:78
  11.3 122.3 %collective-permute-start.2 = (f32[4,768,1]{1,2,0:T(1,128)S(1)}, f32[4,768,1]{1,2,0:T(1,128)S(1)}, u32[]{:S(2)}, u32[]{:S(2)}) collective-permute-start(f32[4,768,1]{1,2,0:T(1,128)S(1)} %get-tuple-element.34), channel_id=1, source_target_pairs={{1,0},{2,1},{3,2},{4,3},{5,4},{6,5},{7,6},{8,7},{9,8},{10,9},{11,1... | collective-permute-start | bytes 36872 | tf_op jit(solution)/shard_map/ppermute | solution.py:27
  13.3 120.3 %collective-permute-start.3 = (f32[4,768,1]{1,2,0:T(1,128)S(1)}, f32[4,768,1]{1,2,0:T(1,128)S(1)}, u32[]{:S(2)}, u32[]{:S(2)}) collective-permute-start(f32[4,768,1]{1,2,0:T(1,128)S(1)} %get-tuple-element.35), channel_id=1, source_target_pairs={{0,1},{1,2},{2,3},{3,4},{4,5},{5,6},{6,7},{7,8},{8,9},{9,10},{10,1... | collective-permute-start | bytes 36872 | tf_op jit(solution)/shard_map/ppermute | solution.py:26
  18.3 115.3 %collective-permute-start.1 = (f32[1,768,128]{1,2,0:T(8,128)S(1)}, f32[1,768,128]{1,2,0:T(8,128)}, u32[]{:S(2)}, u32[]{:S(2)}) collective-permute-start(f32[1,768,128]{1,2,0:T(8,128)S(1)} %get-tuple-element.36), channel_id=1, source_target_pairs={{0,16},{16,32},{32,48},{48,64},{64,80},{80,96},{96,112},{1,17},{17... | collective-permute-start | bytes 1179656 | tf_op jit(solution)/shard_map/ppermute | solution.py:26
  20.2 7.1 %copy-start.19 = (s32[1,4,1]{1,2,0:T(1,128)S(1)}, s32[1,4,1]{1,2,0:T(1,128)}, u32[]{:S(2)}) copy-start(s32[1,4,1]{1,2,0:T(1,128)} %param.12) | copy-start | bytes 52
  20.3 7.1 %copy-start.17 = (s32[4,128]{1,0:T(4,128)S(1)}, s32[4,128]{1,0:T(4,128)}, u32[]{:S(2)}) copy-start(s32[4,128]{1,0:T(4,128)} %param.11) | copy-start | bytes 6148
  20.3 113.3 %collective-permute-start = (f32[1,768,128]{1,2,0:T(8,128)S(1)}, f32[1,768,128]{1,2,0:T(8,128)}, u32[]{:S(2)}, u32[]{:S(2)}) collective-permute-start(f32[1,768,128]{1,2,0:T(8,128)S(1)} %get-tuple-element.37), channel_id=1, source_target_pairs={{16,0},{32,16},{48,32},{64,48},{80,64},{96,80},{112,96},{17,1},{33... | collective-permute-start | bytes 1179656 | tf_op jit(solution)/shard_map/ppermute | solution.py:27
  119.9 13.7 %copy-start.1 = (f32[4,768,128]{1,2,0:T(8,128)S(1)}, f32[4,768,128]{1,2,0:T(8,128)}, u32[]{:S(2)}) copy-start(f32[4,768,128]{1,2,0:T(8,128)} %copy.40) | copy-start | bytes 4718596
  119.9 13.7 %copy-start.15 = (f32[4,768,128]{2,1,0:T(8,128)S(1)}, f32[4,768,128]{2,1,0:T(8,128)}, u32[]{:S(2)}) copy-start(f32[4,768,128]{2,1,0:T(8,128)} %param.7) | copy-start | bytes 4718596
  119.9 13.7 %copy-start.16 = (f32[4,768,128]{1,2,0:T(8,128)S(1)}, f32[4,768,128]{1,2,0:T(8,128)}, u32[]{:S(2)}) copy-start(f32[4,768,128]{1,2,0:T(8,128)} %copy.36) | copy-start | bytes 4718596
  119.9 13.7 %copy-start.18 = (f32[768]{0:T(1024)S(1)}, f32[768]{0:T(1024)}, u32[]{:S(2)}) copy-start(f32[768]{0:T(1024)} %param.10) | copy-start | bytes 9220
  179.7 24.4 %copy-start.9 = (f32[4,768,128]{1,2,0:T(8,128)}, f32[4,768,128]{1,2,0:T(8,128)S(1)}, u32[]{:S(2)}) copy-start(f32[4,768,128]{1,2,0:T(8,128)S(1)} %broadcast_divide_fusion.3) | copy-start | bytes 4718596
  179.7 11.8 %copy-start.2 = (f32[4,768,128]{1,2,0:T(8,128)S(1)}, f32[4,768,128]{1,2,0:T(8,128)}, u32[]{:S(2)}) copy-start(f32[4,768,128]{1,2,0:T(8,128)} %copy.40) | copy-start | bytes 4718596
  179.8 24.3 %collective-permute-start.6 = (f32[4,768,1]{1,2,0:T(1,128)S(1)}, f32[4,768,1]{1,2,0:T(1,128)S(1)}, u32[]{:S(2)}, u32[]{:S(2)}) collective-permute-start(f32[4,768,1]{1,2,0:T(1,128)S(1)} %get-tuple-element.30), channel_id=1, source_target_pairs={{1,0},{2,1},{3,2},{4,3},{5,4},{6,5},{7,6},{8,7},{9,8},{10,9},{11,1... | collective-permute-start | bytes 36872 | tf_op jit(solution)/shard_map/ppermute | solution.py:27
  183.5 20.6 %collective-permute-start.7 = (f32[4,768,1]{1,2,0:T(1,128)S(1)}, f32[4,768,1]{1,2,0:T(1,128)S(1)}, u32[]{:S(2)}, u32[]{:S(2)}) collective-permute-start(f32[4,768,1]{1,2,0:T(1,128)S(1)} %get-tuple-element.31), channel_id=1, source_target_pairs={{0,1},{1,2},{2,3},{3,4},{4,5},{5,6},{6,7},{7,8},{8,9},{9,10},{10,1... | collective-permute-start | bytes 36872 | tf_op jit(solution)/shard_map/ppermute | solution.py:26
  185.9 18.2 %collective-permute-start.5 = (f32[1,768,128]{1,2,0:T(8,128)S(1)}, f32[1,768,128]{1,2,0:T(8,128)S(1)}, u32[]{:S(2)}, u32[]{:S(2)}) collective-permute-start(f32[1,768,128]{1,2,0:T(8,128)S(1)} %get-tuple-element.32), channel_id=1, source_target_pairs={{0,16},{16,32},{32,48},{48,64},{64,80},{80,96},{96,112},{1,17},{17... | collective-permute-start | bytes 1179656 | tf_op jit(solution)/shard_map/ppermute | solution.py:26
  187.8 16.3 %collective-permute-start.4 = (f32[1,768,128]{1,2,0:T(8,128)S(1)}, f32[1,768,128]{1,2,0:T(8,128)S(1)}, u32[]{:S(2)}, u32[]{:S(2)}) collective-permute-start(f32[1,768,128]{1,2,0:T(8,128)S(1)} %get-tuple-element.33), channel_id=1, source_target_pairs={{16,0},{32,16},{48,32},{64,48},{80,64},{96,80},{112,96},{17,1},{33... | collective-permute-start | bytes 1179656 | tf_op jit(solution)/shard_map/ppermute | solution.py:27
  282.0 25.0 %copy-start.6 = (f32[4,768,128]{1,2,0:T(8,128)}, f32[4,768,128]{1,2,0:T(8,128)S(1)}, u32[]{:S(2)}) copy-start(f32[4,768,128]{1,2,0:T(8,128)S(1)} %broadcast_divide_fusion.2) | copy-start | bytes 4718596
  282.0 12.3 %copy-start.3 = (f32[4,768,128]{1,2,0:T(8,128)S(1)}, f32[4,768,128]{1,2,0:T(8,128)}, u32[]{:S(2)}) copy-start(f32[4,768,128]{1,2,0:T(8,128)} %copy.40) | copy-start | bytes 4718596
  282.1 24.8 %collective-permute-start.10 = (f32[4,768,1]{1,2,0:T(1,128)S(1)}, f32[4,768,1]{1,2,0:T(1,128)S(1)}, u32[]{:S(2)}, u32[]{:S(2)}) collective-permute-start(f32[4,768,1]{1,2,0:T(1,128)S(1)} %get-tuple-element.26), channel_id=1, source_target_pairs={{1,0},{2,1},{3,2},{4,3},{5,4},{6,5},{7,6},{8,7},{9,8},{10,9},{11,1... | collective-permute-start | bytes 36872 | tf_op jit(solution)/shard_map/ppermute | solution.py:27
  284.3 22.6 %collective-permute-start.11 = (f32[4,768,1]{1,2,0:T(1,128)S(1)}, f32[4,768,1]{1,2,0:T(1,128)S(1)}, u32[]{:S(2)}, u32[]{:S(2)}) collective-permute-start(f32[4,768,1]{1,2,0:T(1,128)S(1)} %get-tuple-element.27), channel_id=1, source_target_pairs={{0,1},{1,2},{2,3},{3,4},{4,5},{5,6},{6,7},{7,8},{8,9},{9,10},{10,1... | collective-permute-start | bytes 36872 | tf_op jit(solution)/shard_map/ppermute | solution.py:26
  288.2 18.7 %collective-permute-start.9 = (f32[1,768,128]{1,2,0:T(8,128)S(1)}, f32[1,768,128]{1,2,0:T(8,128)S(1)}, u32[]{:S(2)}, u32[]{:S(2)}) collective-permute-start(f32[1,768,128]{1,2,0:T(8,128)S(1)} %get-tuple-element.28), channel_id=1, source_target_pairs={{0,16},{16,32},{32,48},{48,64},{64,80},{80,96},{96,112},{1,17},{17... | collective-permute-start | bytes 1179656 | tf_op jit(solution)/shard_map/ppermute | solution.py:26
  290.2 16.8 %copy-start.10 = (f32[4,768,128]{1,2,0:T(8,128)S(1)}, f32[4,768,128]{1,2,0:T(8,128)}, u32[]{:S(2)}) copy-start(f32[4,768,128]{1,2,0:T(8,128)} %copy-done.9) | copy-start | bytes 4718596
  290.2 16.8 %collective-permute-start.8 = (f32[1,768,128]{1,2,0:T(8,128)S(1)}, f32[1,768,128]{1,2,0:T(8,128)S(1)}, u32[]{:S(2)}, u32[]{:S(2)}) collective-permute-start(f32[1,768,128]{1,2,0:T(8,128)S(1)} %get-tuple-element.29), channel_id=1, source_target_pairs={{16,0},{32,16},{48,32},{64,48},{80,64},{96,80},{112,96},{17,1},{33... | collective-permute-start | bytes 1179656 | tf_op jit(solution)/shard_map/ppermute | solution.py:27
  385.7 24.9 %copy-start.13 = (f32[4,768,128]{1,2,0:T(8,128)}, f32[4,768,128]{1,2,0:T(8,128)S(1)}, u32[]{:S(2)}) copy-start(f32[4,768,128]{1,2,0:T(8,128)S(1)} %broadcast_divide_fusion.1) | copy-start | bytes 4718596
  385.7 12.3 %copy-start.4 = (f32[4,768,128]{1,2,0:T(8,128)S(1)}, f32[4,768,128]{1,2,0:T(8,128)}, u32[]{:S(2)}) copy-start(f32[4,768,128]{1,2,0:T(8,128)} %copy.40) | copy-start | bytes 4718596
  385.8 24.7 %collective-permute-start.14 = (f32[4,768,1]{1,2,0:T(1,128)S(1)}, f32[4,768,1]{1,2,0:T(1,128)S(1)}, u32[]{:S(2)}, u32[]{:S(2)}) collective-permute-start(f32[4,768,1]{1,2,0:T(1,128)S(1)} %get-tuple-element.22), channel_id=1, source_target_pairs={{1,0},{2,1},{3,2},{4,3},{5,4},{6,5},{7,6},{8,7},{9,8},{10,9},{11,1... | collective-permute-start | bytes 36872 | tf_op jit(solution)/shard_map/ppermute | solution.py:27
  388.0 22.5 %collective-permute-start.15 = (f32[4,768,1]{1,2,0:T(1,128)S(1)}, f32[4,768,1]{1,2,0:T(1,128)S(1)}, u32[]{:S(2)}, u32[]{:S(2)}) collective-permute-start(f32[4,768,1]{1,2,0:T(1,128)S(1)} %get-tuple-element.23), channel_id=1, source_target_pairs={{0,1},{1,2},{2,3},{3,4},{4,5},{5,6},{6,7},{7,8},{8,9},{9,10},{10,1... | collective-permute-start | bytes 36872 | tf_op jit(solution)/shard_map/ppermute | solution.py:26
  391.9 18.6 %collective-permute-start.13 = (f32[1,768,128]{1,2,0:T(8,128)S(1)}, f32[1,768,128]{1,2,0:T(8,128)S(1)}, u32[]{:S(2)}, u32[]{:S(2)}) collective-permute-start(f32[1,768,128]{1,2,0:T(8,128)S(1)} %get-tuple-element.24), channel_id=1, source_target_pairs={{0,16},{16,32},{32,48},{48,64},{64,80},{80,96},{96,112},{1,17},{17... | collective-permute-start | bytes 1179656 | tf_op jit(solution)/shard_map/ppermute | solution.py:26
  393.9 16.7 %copy-start.7 = (f32[4,768,128]{1,2,0:T(8,128)S(1)}, f32[4,768,128]{1,2,0:T(8,128)}, u32[]{:S(2)}) copy-start(f32[4,768,128]{1,2,0:T(8,128)} %copy-done.6) | copy-start | bytes 4718596
  393.9 16.7 %copy-start.11 = (f32[4,768,128]{1,2,0:T(8,128)S(1)}, f32[4,768,128]{1,2,0:T(8,128)}, u32[]{:S(2)}) copy-start(f32[4,768,128]{1,2,0:T(8,128)} %copy-done.9) | copy-start | bytes 4718596
  393.9 16.7 %collective-permute-start.12 = (f32[1,768,128]{1,2,0:T(8,128)S(1)}, f32[1,768,128]{1,2,0:T(8,128)S(1)}, u32[]{:S(2)}, u32[]{:S(2)}) collective-permute-start(f32[1,768,128]{1,2,0:T(8,128)S(1)} %get-tuple-element.25), channel_id=1, source_target_pairs={{16,0},{32,16},{48,32},{64,48},{80,64},{96,80},{112,96},{17,1},{33... | collective-permute-start | bytes 1179656 | tf_op jit(solution)/shard_map/ppermute | solution.py:27
  491.6 12.2 %copy-start.5 = (f32[4,768,128]{1,2,0:T(8,128)S(1)}, f32[4,768,128]{1,2,0:T(8,128)}, u32[]{:S(2)}) copy-start(f32[4,768,128]{1,2,0:T(8,128)} %copy.40) | copy-start | bytes 4718596
  491.7 24.7 %collective-permute-start.18 = (f32[4,768,1]{1,2,0:T(1,128)S(1)}, f32[4,768,1]{1,2,0:T(1,128)S(1)}, u32[]{:S(2)}, u32[]{:S(2)}) collective-permute-start(f32[4,768,1]{1,2,0:T(1,128)S(1)} %get-tuple-element.18), channel_id=1, source_target_pairs={{1,0},{2,1},{3,2},{4,3},{5,4},{6,5},{7,6},{8,7},{9,8},{10,9},{11,1... | collective-permute-start | bytes 36872 | tf_op jit(solution)/shard_map/ppermute | solution.py:27
  493.7 22.6 %collective-permute-start.19 = (f32[4,768,1]{1,2,0:T(1,128)S(1)}, f32[4,768,1]{1,2,0:T(1,128)S(1)}, u32[]{:S(2)}, u32[]{:S(2)}) collective-permute-start(f32[4,768,1]{1,2,0:T(1,128)S(1)} %get-tuple-element.19), channel_id=1, source_target_pairs={{0,1},{1,2},{2,3},{3,4},{4,5},{5,6},{6,7},{7,8},{8,9},{9,10},{10,1... | collective-permute-start | bytes 36872 | tf_op jit(solution)/shard_map/ppermute | solution.py:26
  497.7 18.7 %collective-permute-start.17 = (f32[1,768,128]{1,2,0:T(8,128)S(1)}, f32[1,768,128]{1,2,0:T(8,128)S(1)}, u32[]{:S(2)}, u32[]{:S(2)}) collective-permute-start(f32[1,768,128]{1,2,0:T(8,128)S(1)} %get-tuple-element.20), channel_id=1, source_target_pairs={{0,16},{16,32},{32,48},{48,64},{64,80},{80,96},{96,112},{1,17},{17... | collective-permute-start | bytes 1179656 | tf_op jit(solution)/shard_map/ppermute | solution.py:26
  499.6 16.8 %copy-start.8 = (f32[4,768,128]{1,2,0:T(8,128)S(1)}, f32[4,768,128]{1,2,0:T(8,128)}, u32[]{:S(2)}) copy-start(f32[4,768,128]{1,2,0:T(8,128)} %copy-done.6) | copy-start | bytes 4718596
  499.6 16.8 %copy-start.12 = (f32[4,768,128]{1,2,0:T(8,128)S(1)}, f32[4,768,128]{1,2,0:T(8,128)}, u32[]{:S(2)}) copy-start(f32[4,768,128]{1,2,0:T(8,128)} %copy-done.9) | copy-start | bytes 4718596
  499.6 16.8 %copy-start.14 = (f32[4,768,128]{1,2,0:T(8,128)S(1)}, f32[4,768,128]{1,2,0:T(8,128)}, u32[]{:S(2)}) copy-start(f32[4,768,128]{1,2,0:T(8,128)} %copy-done.13) | copy-start | bytes 4718596
  499.6 16.7 %collective-permute-start.16 = (f32[1,768,128]{1,2,0:T(8,128)S(1)}, f32[1,768,128]{1,2,0:T(8,128)S(1)}, u32[]{:S(2)}, u32[]{:S(2)}) collective-permute-start(f32[1,768,128]{1,2,0:T(8,128)S(1)} %get-tuple-element.21), channel_id=1, source_target_pairs={{16,0},{32,16},{48,32},{64,48},{80,64},{96,80},{112,96},{17,1},{33... | collective-permute-start | bytes 1179656 | tf_op jit(solution)/shard_map/ppermute | solution.py:27
Sparse Core Ops, SparseCore 0:
  9.0 99.6 all-gather.1
where the time goes:
time: 643 us; the launch traced here: 631 us
  blocking collectives  283 us (44%)
  matrix products  103 us (16%)
  waiting for transfers between devices  82.1 us (13%)
  starting transfers between devices  59.5 us (9%)
  other arithmetic  44.2 us (7%)
  between operations  33.5 us (5%)
  local copies, waits for them, and re-layouts  26.4 us (4%)
    psum x36, blocking collectives, one_axis_at_a_time(): return functools.reduce(lax.psum, axes, array)  283 us
    all_gather x1, waiting for transfers between devices, local(): every_op = lax.all_gather(correction_ops, GX, axis=0, tiled=True)  81.3 us
    dot_general x5, matrix products, correct(): jnp.einsum('bpq,bqc->bpc', chosen, field, precision=highest) * weights  63.9 us
    dot_general x5, matrix products, spread(): mixed = jnp.einsum('pq,xqy->xpy', vertical_mix, field, precision=highest)  38.6 us
    ppermute x10, starting transfers between devices, padded_2(): lax.ppermute(first, axis, [(b, a) for a, b in up])  31.9 us
    ppermute x10, starting transfers between devices, padded_2(): lax.ppermute(last, axis, up)  27.6 us
    reduce_sum x4, other arithmetic, squares(): return one_axis_at_a_time(jnp.sum(field * field), GX_GY)  23.4 us
  transfers between devices with their start and end apart: 21, of which 1 were waited for; matrix products, arithmetic and copies ran while one was open for 13% of the time, Pallas kernels for 0%

commit v1 on v0

--- a/solution.py
+++ b/solution.py
@@ -75,7 +75,9 @@
         mixed = jnp.einsum("pq,xqy->xpy", vertical_mix, field, precision=highest)
         return 2.0 * field + mixed + coeff_rows * lap
 
-    every_op = lax.all_gather(correction_ops, GX, axis=0, tiled=True)
+    every_op = jnp.concatenate(
+        lax.all_to_all(jnp.stack([correction_ops] * lax.axis_size(GX)), GX, 0, 0), axis=0
+    )
     chosen = every_op[regimes]
 
     def correct(field):

time: 643 us -> 739 us (1.15); the launches traced: 631 us -> 735 us
  waiting for transfers between devices: 82.1 us -> 187 us
  between operations: 33.5 us -> 19.6 us
  local copies, waits for them, and re-layouts: 26.4 us -> 35.9 us
    all_to_all x0 -> x1, waiting for transfers between devices: none -> 187 us  [local(): lax.all_to_all(jnp.stack([correction_ops] * lax.axis_size(GX)), GX, 0, 0)]
    all_gather x1 -> x0, waiting for transfers between devices: 81.3 us -> none  [local(): every_op = lax.all_gather(correction_ops, GX, axis=0, tiled=True)]
    another operation x2 -> x3, local copies, waits for them, and re-layouts: 0.01 us -> 9.89 us  [the longest x1 9.89 us: local(): jnp.stack([correction_ops] * lax.axis_size(GX))]
    ppermute x10, starting transfers between devices: 31.9 us -> 23.2 us  [padded_2(): lax.ppermute(first, axis, [(b, a) for a, b in up])]
  transfers between devices with their start and end apart: 21 -> 21, of which waited for: 1 -> 1; matrix products, arithmetic and copies ran while one was open for 13% -> 11% of each run, Pallas kernels for 0% -> 0%
where the time goes in v1:
time: 739 us; the launch traced here: 735 us
  blocking collectives  285 us (39%)
  waiting for transfers between devices  187 us (25%)
  matrix products  103 us (14%)
  starting transfers between devices  60.4 us (8%)
  other arithmetic  44.1 us (6%)
  local copies, waits for them, and re-layouts  35.9 us (5%)
  between operations  19.6 us (3%)
    psum x36, blocking collectives, one_axis_at_a_time(): return functools.reduce(lax.psum, axes, array)  285 us
    all_to_all x1, waiting for transfers between devices, local(): lax.all_to_all(jnp.stack([correction_ops] * lax.axis_size(GX)), GX, 0, 0)  187 us
    dot_general x5, matrix products, correct(): jnp.einsum('bpq,bqc->bpc', chosen, field, precision=highest) * weights  63.9 us
    dot_general x5, matrix products, spread(): mixed = jnp.einsum('pq,xqy->xpy', vertical_mix, field, precision=highest)  38.6 us
    ppermute x10, starting transfers between devices, padded_2(): lax.ppermute(last, axis, up)  30.9 us
    reduce_sum x4, other arithmetic, squares(): return one_axis_at_a_time(jnp.sum(field * field), GX_GY)  23.3 us
    ppermute x10, starting transfers between devices, padded_2(): lax.ppermute(first, axis, [(b, a) for a, b in up])  23.2 us
  transfers between devices with their start and end apart: 21, of which 1 were waited for; matrix products, arithmetic and copies ran while one was open for 11% of the time, Pallas kernels for 0%

profile of v1, /device:TPU:34, one launch (start us, length us, event | category | flops | bytes accessed | tf_op | source)
XLA Modules:
  0.0 734.8 jit_solution(16471709997994042430)
XLA Ops:
  0.0 9.9 %stack.65 = f32[8,1,768,768]{3,2,1,0:T(8,128)} broadcast(f32[768,768]{1,0:T(8,128)} %bitcast.117), dimensions={2,3} | broadcast | bytes 21233664 | tf_op jit(solution)/shard_map/stack | solution.py:79
  9.9 6.3 all-to-all-start
  34.9 187.1 %all-to-all-done = f32[8,1,768,768]{3,2,1,0:T(8,128)} async-done(((f32[8,1,768,768]{3,2,1,0:T(8,128)}), f32[8,1,768,768]{3,2,1,0:T(8,128)}, u32[]{:S(2)}, u32[]{:S(2)}) %all-to-all-start) | async-done | bytes 18874400 | tf_op jit(solution)/shard_map/all_to_all | solution.py:79
  221.9 11.2 %gather_fusion = f32[4,768,768]{2,1,0:T(8,128)} fusion(f32[8,768,768]{2,1,0:T(8,128)} %bitcast.3, s32[1024]{0:T(1024)S(1)} %pad_clamp_fusion), kind=kCustom, calls=%fused_computation | custom fusion | bytes 18874384 | tf_op jit(solution)/shard_map/gather | solution.py:81
  233.2 13.7 %fusion.74 = f32[4,768,128]{1,2,0:T(8,128)S(1)} fusion(f32[4,768,768]{2,1,0:T(8,128)} %gather_fusion, f32[4,768,128]{1,2,0:T(8,128)} %copy.23), kind=kOutput, calls=%fused_computation.132 | convolution fusion | flops 3623878656 | bytes 12582912 | tf_op jit(solution)/shard_map/bpq,bqc->bpc/dot_general | solution.py:84
  247.0 11.3 %multiply_reduce_fusion.14 = (f32[]{:T(128)}, f32[4,768,128]{1,2,0:T(8,128)}) fusion(f32[4,768,128]{1,2,0:T(8,128)S(1)} %copy-done.16, f32[4,768,128]{1,2,0:T(8,128)S(1)} %fusion.74, f32[4,128]{1,0:T(4,128)S(1)} %convert_multiply_fusion, f32[1,768,128]{1,2,0:T(8,128)} %collective-permute-done, f32[4,768,128]{1,2,0:T(8,128)S(1)} %copy-done.1, ...), kind=kOutput, calls=%fused_computation.131 | convolution fusion | flops 3634888704 | bytes 11039748 | tf_op jit(solution)/shard_map/pq,xqy->xpy/dot_general | solution.py:75
  258.3 10.3 %psum.252 = f32[]{:T(128)} all-reduce(f32[]{:T(128)} %get-tuple-element.61), channel_id=1, replica_groups=mesh['gx_0'=4,'gx_1'=2,'gy_0'=4,'gy_1'=4] {'gx_0'}, use_global_device_ids=true, to_apply=%region_1.2 | all-reduce | flops 1 | bytes 8 | tf_op jit(solution)/shard_map/psum | solution.py:15
  271.7 11.6 %psum.254 = f32[]{:T(128)} all-reduce(f32[]{:T(128)} %psum.253), channel_id=1, replica_groups=mesh['gx_0'=4,'gx_1'=2,'gy_0'=4,'gy_1'=4] {'gy_0'}, use_global_device_ids=true, to_apply=%region_3.4 | all-reduce | flops 1 | bytes 8 | tf_op jit(solution)/shard_map/psum | solution.py:15
  283.3 9.7 %psum.255 = f32[]{:T(128)} all-reduce(f32[]{:T(128)} %psum.254), channel_id=1, replica_groups=mesh['gx_0'=4,'gx_1'=2,'gy_0'=4,'gy_1'=4] {'gy_1'}, use_global_device_ids=true, to_apply=%region_4.5 | all-reduce | flops 1 | bytes 8 | tf_op jit(solution)/shard_map/psum | solution.py:15
  299.9 4.7 collective-permute-start.6
  306.6 12.6 %fusion.62 = f32[4,768,128]{1,2,0:T(8,128)S(1)} fusion(f32[4,768,768]{2,1,0:T(8,128)} %gather_fusion, f32[4,768,128]{1,2,0:T(8,128)S(1)} %broadcast_divide_fusion.3, f32[4,768,128]{1,2,0:T(8,128)S(1)} %copy-done.2), kind=kOutput, calls=%fused_computation.128 | convolution fusion | flops 3625058304 | bytes 14155776 | tf_op jit(solution)/shard_map/bpq,bqc->bpc/dot_general | solution.py:84
  319.2 6.6 multiply_reduce_fusion.13
  325.8 8.9 %psum.256 = f32[1]{0:T(128)} all-reduce(f32[1]{0:T(128)} %bitcast.7), channel_id=1, replica_groups=mesh['gx_0'=4,'gx_1'=2,'gy_0'=4,'gy_1'=4] {'gx_0'}, use_global_device_ids=true, to_apply=%region_6.7 | all-reduce | flops 1 | bytes 8 | tf_op jit(solution)/shard_map/psum | solution.py:15
  337.8 8.3 %psum.258 = f32[1]{0:T(128)} all-reduce(f32[1]{0:T(128)} %psum.257), channel_id=1, replica_groups=mesh['gx_0'=4,'gx_1'=2,'gy_0'=4,'gy_1'=4] {'gy_0'}, use_global_device_ids=true, to_apply=%region_8.9 | all-reduce | flops 1 | bytes 8 | tf_op jit(solution)/shard_map/psum | solution.py:15
  346.2 10.3 %psum.259 = f32[1]{0:T(128)} all-reduce(f32[1]{0:T(128)} %psum.258), channel_id=1, replica_groups=mesh['gx_0'=4,'gx_1'=2,'gy_0'=4,'gy_1'=4] {'gy_1'}, use_global_device_ids=true, to_apply=%region_9.10 | all-reduce | flops 1 | bytes 8 | tf_op jit(solution)/shard_map/psum | solution.py:15
  360.0 9.9 %psum.260 = f32[]{:T(128)} all-reduce(f32[]{:T(128)} %multiply_reduce_fusion.12), channel_id=1, replica_groups=mesh['gx_0'=4,'gx_1'=2,'gy_0'=4,'gy_1'=4] {'gx_0'}, use_global_device_ids=true, to_apply=%region_11.12 | all-reduce | flops 1 | bytes 8 | tf_op jit(solution)/shard_map/psum | solution.py:15
  373.0 10.4 %psum.262 = f32[]{:T(128)} all-reduce(f32[]{:T(128)} %psum.261), channel_id=1, replica_groups=mesh['gx_0'=4,'gx_1'=2,'gy_0'=4,'gy_1'=4] {'gy_0'}, use_global_device_ids=true, to_apply=%region_13.14 | all-reduce | flops 1 | bytes 8 | tf_op jit(solution)/shard_map/psum | solution.py:15
  383.5 10.3 %psum.263 = f32[]{:T(128)} all-reduce(f32[]{:T(128)} %psum.262), channel_id=1, replica_groups=mesh['gx_0'=4,'gx_1'=2,'gy_0'=4,'gy_1'=4] {'gy_1'}, use_global_device_ids=true, to_apply=%region_14.15 | all-reduce | flops 1 | bytes 8 | tf_op jit(solution)/shard_map/psum | solution.py:15
  408.1 12.6 %fusion.60 = f32[4,768,128]{1,2,0:T(8,128)S(1)} fusion(f32[4,768,768]{2,1,0:T(8,128)} %gather_fusion, f32[4,768,128]{1,2,0:T(8,128)S(1)} %broadcast_divide_fusion.2, f32[4,768,128]{1,2,0:T(8,128)S(1)} %copy-done.3), kind=kOutput, calls=%fused_computation.123 | convolution fusion | flops 3625058304 | bytes 14155776 | tf_op jit(solution)/shard_map/bpq,bqc->bpc/dot_general | solution.py:84
  420.7 6.8 multiply_reduce_fusion.11
  428.8 8.3 %psum.264 = f32[2]{0:T(128)S(1)} all-reduce(f32[2]{0:T(128)S(1)} %pad_maximum_fusion.31), channel_id=1, replica_groups=mesh['gx_0'=4,'gx_1'=2,'gy_0'=4,'gy_1'=4] {'gx_0'}, use_global_device_ids=true, to_apply=%region_17.18 | all-reduce | flops 2 | bytes 16 | tf_op jit(solution)/shard_map/psum | solution.py:15
  439.5 7.7 %psum.266 = f32[2]{0:T(128)S(1)} all-reduce(f32[2]{0:T(128)S(1)} %psum.265), channel_id=1, replica_groups=mesh['gx_0'=4,'gx_1'=2,'gy_0'=4,'gy_1'=4] {'gy_0'}, use_global_device_ids=true, to_apply=%region_19.20 | all-reduce | flops 2 | bytes 16 | tf_op jit(solution)/shard_map/psum | solution.py:15
  447.3 9.2 %psum.267 = f32[2]{0:T(128)S(1)} all-reduce(f32[2]{0:T(128)S(1)} %psum.266), channel_id=1, replica_groups=mesh['gx_0'=4,'gx_1'=2,'gy_0'=4,'gy_1'=4] {'gy_1'}, use_global_device_ids=true, to_apply=%region_20.21 | all-reduce | flops 2 | bytes 16 | tf_op jit(solution)/shard_map/psum | solution.py:15
  457.0 5.7 multiply_reduce_fusion.9
  462.8 9.8 %psum.268 = f32[]{:T(128)} all-reduce(f32[]{:T(128)} %get-tuple-element.16), channel_id=1, replica_groups=mesh['gx_0'=4,'gx_1'=2,'gy_0'=4,'gy_1'=4] {'gx_0'}, use_global_device_ids=true, to_apply=%region_22.23 | all-reduce | flops 1 | bytes 8 | tf_op jit(solution)/shard_map/psum | solution.py:15
  475.7 9.8 %psum.270 = f32[]{:T(128)} all-reduce(f32[]{:T(128)} %psum.269), channel_id=1, replica_groups=mesh['gx_0'=4,'gx_1'=2,'gy_0'=4,'gy_1'=4] {'gy_0'}, use_global_device_ids=true, to_apply=%region_24.25 | all-reduce | flops 1 | bytes 8 | tf_op jit(solution)/shard_map/psum | solution.py:15
  485.5 11.6 %psum.271 = f32[]{:T(128)} all-reduce(f32[]{:T(128)} %psum.270), channel_id=1, replica_groups=mesh['gx_0'=4,'gx_1'=2,'gy_0'=4,'gy_1'=4] {'gy_1'}, use_global_device_ids=true, to_apply=%region_25.26 | all-reduce | flops 1 | bytes 8 | tf_op jit(solution)/shard_map/psum | solution.py:15
  506.0 4.4 collective-permute-start.15
  510.4 12.6 %fusion.58 = f32[4,768,128]{1,2,0:T(8,128)S(1)} fusion(f32[4,768,768]{2,1,0:T(8,128)} %gather_fusion, f32[4,768,128]{1,2,0:T(8,128)S(1)} %broadcast_divide_fusion.1, f32[4,768,128]{1,2,0:T(8,128)S(1)} %copy-done.4), kind=kOutput, calls=%fused_computation.117 | convolution fusion | flops 3625058304 | bytes 14155776 | tf_op jit(solution)/shard_map/bpq,bqc->bpc/dot_general | solution.py:84
  523.0 6.9 multiply_reduce_fusion.8
  532.0 8.3 %psum.272 = f32[3]{0:T(128)S(1)} all-reduce(f32[3]{0:T(128)S(1)} %pad_maximum_fusion.32), channel_id=1, replica_groups=mesh['gx_0'=4,'gx_1'=2,'gy_0'=4,'gy_1'=4] {'gx_0'}, use_global_device_ids=true, to_apply=%region_29.30 | all-reduce | flops 3 | bytes 24 | tf_op jit(solution)/shard_map/psum | solution.py:15
  542.7 7.7 %psum.274 = f32[3]{0:T(128)S(1)} all-reduce(f32[3]{0:T(128)S(1)} %psum.273), channel_id=1, replica_groups=mesh['gx_0'=4,'gx_1'=2,'gy_0'=4,'gy_1'=4] {'gy_0'}, use_global_device_ids=true, to_apply=%region_31.32 | all-reduce | flops 3 | bytes 24 | tf_op jit(solution)/shard_map/psum | solution.py:15
  550.5 9.2 %psum.275 = f32[3]{0:T(128)S(1)} all-reduce(f32[3]{0:T(128)S(1)} %psum.274), channel_id=1, replica_groups=mesh['gx_0'=4,'gx_1'=2,'gy_0'=4,'gy_1'=4] {'gy_1'}, use_global_device_ids=true, to_apply=%region_32.33 | all-reduce | flops 3 | bytes 24 | tf_op jit(solution)/shard_map/psum | solution.py:15
  560.3 7.0 multiply_reduce_fusion.5
  567.3 9.8 %psum.276 = f32[]{:T(128)} all-reduce(f32[]{:T(128)} %get-tuple-element.14), channel_id=1, replica_groups=mesh['gx_0'=4,'gx_1'=2,'gy_0'=4,'gy_1'=4] {'gx_0'}, use_global_device_ids=true, to_apply=%region_34.35 | all-reduce | flops 1 | bytes 8 | tf_op jit(solution)/shard_map/psum | solution.py:15
  580.2 9.9 %psum.278 = f32[]{:T(128)} all-reduce(f32[]{:T(128)} %psum.277), channel_id=1, replica_groups=mesh['gx_0'=4,'gx_1'=2,'gy_0'=4,'gy_1'=4] {'gy_0'}, use_global_device_ids=true, to_apply=%region_36.37 | all-reduce | flops 1 | bytes 8 | tf_op jit(solution)/shard_map/psum | solution.py:15
  590.1 11.6 %psum.279 = f32[]{:T(128)} all-reduce(f32[]{:T(128)} %psum.278), channel_id=1, replica_groups=mesh['gx_0'=4,'gx_1'=2,'gy_0'=4,'gy_1'=4] {'gy_1'}, use_global_device_ids=true, to_apply=%region_37.38 | all-reduce | flops 1 | bytes 8 | tf_op jit(solution)/shard_map/psum | solution.py:15
  610.5 4.4 collective-permute-start.19
  614.9 12.6 %fusion.56 = f32[4,768,128]{1,2,0:T(8,128)S(1)} fusion(f32[4,768,768]{2,1,0:T(8,128)} %gather_fusion, f32[4,768,128]{1,2,0:T(8,128)S(1)} %broadcast_divide_fusion, f32[4,768,128]{1,2,0:T(8,128)S(1)} %copy-done.5), kind=kOutput, calls=%fused_computation.110 | convolution fusion | flops 3625058304 | bytes 14155776 | tf_op jit(solution)/shard_map/bpq,bqc->bpc/dot_general | solution.py:84
  627.5 7.0 multiply_reduce_fusion.4
  637.0 8.3 %psum.280 = f32[4]{0:T(128)S(1)} all-reduce(f32[4]{0:T(128)S(1)} %pad_maximum_fusion.33), channel_id=1, replica_groups=mesh['gx_0'=4,'gx_1'=2,'gy_0'=4,'gy_1'=4] {'gx_0'}, use_global_device_ids=true, to_apply=%region_42.43 | all-reduce | flops 4 | bytes 32 | tf_op jit(solution)/shard_map/psum | solution.py:15
  647.8 7.7 %psum.282 = f32[4]{0:T(128)S(1)} all-reduce(f32[4]{0:T(128)S(1)} %psum.281), channel_id=1, replica_groups=mesh['gx_0'=4,'gx_1'=2,'gy_0'=4,'gy_1'=4] {'gy_0'}, use_global_device_ids=true, to_apply=%region_44.45 | all-reduce | flops 4 | bytes 32 | tf_op jit(solution)/shard_map/psum | solution.py:15
  655.5 9.2 %psum.283 = f32[4]{0:T(128)S(1)} all-reduce(f32[4]{0:T(128)S(1)} %psum.282), channel_id=1, replica_groups=mesh['gx_0'=4,'gx_1'=2,'gy_0'=4,'gy_1'=4] {'gy_1'}, use_global_device_ids=true, to_apply=%region_45.46 | all-reduce | flops 4 | bytes 32 | tf_op jit(solution)/shard_map/psum | solution.py:15
  665.3 7.0 multiply_reduce_fusion
  672.3 9.8 %psum.284 = f32[]{:T(128)} all-reduce(f32[]{:T(128)} %multiply_reduce_fusion), channel_id=1, replica_groups=mesh['gx_0'=4,'gx_1'=2,'gy_0'=4,'gy_1'=4] {'gx_0'}, use_global_device_ids=true, to_apply=%region_47.48 | all-reduce | flops 1 | bytes 8 | tf_op jit(solution)/shard_map/psum | solution.py:15
  685.9 9.8 %psum.286 = f32[]{:T(128)} all-reduce(f32[]{:T(128)} %psum.285), channel_id=1, replica_groups=mesh['gx_0'=4,'gx_1'=2,'gy_0'=4,'gy_1'=4] {'gy_0'}, use_global_device_ids=true, to_apply=%region_49.50 | all-reduce | flops 1 | bytes 8 | tf_op jit(solution)/shard_map/psum | solution.py:15
  695.8 11.6 %psum.287 = f32[]{:T(128)} all-reduce(f32[]{:T(128)} %psum.286), channel_id=1, replica_groups=mesh['gx_0'=4,'gx_1'=2,'gy_0'=4,'gy_1'=4] {'gy_1'}, use_global_device_ids=true, to_apply=%region_50.51 | all-reduce | flops 1 | bytes 8 | tf_op jit(solution)/shard_map/psum | solution.py:15
  726.3 5.0 multiply_add_fusion
  (130 shorter events, 100.9 us)
Async XLA Ops:
  0.0 246.9 %copy-start = (f32[768,768]{1,0:T(8,128)S(1)}, f32[768,768]{1,0:T(8,128)}, u32[]{:S(2)}) copy-start(f32[768,768]{1,0:T(8,128)} %param.9) | copy-start | bytes 7077892
  9.9 212.0 %all-to-all-start = ((f32[8,1,768,768]{3,2,1,0:T(8,128)}), f32[8,1,768,768]{3,2,1,0:T(8,128)}, u32[]{:S(2)}, u32[]{:S(2)}) async-start(f32[8,1,768,768]{3,2,1,0:T(8,128)} %stack.65), calls=%async_computation | async-start | bytes 37748736 | tf_op jit(solution)/shard_map/all_to_all | solution.py:79
  20.4 226.5 %collective-permute-start = (f32[1,768,128]{1,2,0:T(8,128)S(1)}, f32[1,768,128]{1,2,0:T(8,128)}, u32[]{:S(2)}, u32[]{:S(2)}) collective-permute-start(f32[1,768,128]{1,2,0:T(8,128)S(1)} %get-tuple-element.37), channel_id=1, source_target_pairs={{16,0},{32,16},{48,32},{64,48},{80,64},{96,80},{112,96},{17,1},{33... | collective-permute-start | bytes 1179656 | tf_op jit(solution)/shard_map/ppermute | solution.py:27
  22.4 224.5 %collective-permute-start.1 = (f32[1,768,128]{1,2,0:T(8,128)S(1)}, f32[1,768,128]{1,2,0:T(8,128)}, u32[]{:S(2)}, u32[]{:S(2)}) collective-permute-start(f32[1,768,128]{1,2,0:T(8,128)S(1)} %get-tuple-element.36), channel_id=1, source_target_pairs={{0,16},{16,32},{32,48},{48,64},{64,80},{80,96},{96,112},{1,17},{17... | collective-permute-start | bytes 1179656 | tf_op jit(solution)/shard_map/ppermute | solution.py:26
  25.7 221.2 %collective-permute-start.2 = (f32[4,768,1]{1,2,0:T(1,128)S(1)}, f32[4,768,1]{1,2,0:T(1,128)S(1)}, u32[]{:S(2)}, u32[]{:S(2)}) collective-permute-start(f32[4,768,1]{1,2,0:T(1,128)S(1)} %get-tuple-element.34), channel_id=1, source_target_pairs={{1,0},{2,1},{3,2},{4,3},{5,4},{6,5},{7,6},{8,7},{9,8},{10,9},{11,1... | collective-permute-start | bytes 36872 | tf_op jit(solution)/shard_map/ppermute | solution.py:27
  27.6 7.2 copy-start.19
  27.7 7.2 copy-start.17
  27.7 219.2 %collective-permute-start.3 = (f32[4,768,1]{1,2,0:T(1,128)S(1)}, f32[4,768,1]{1,2,0:T(1,128)S(1)}, u32[]{:S(2)}, u32[]{:S(2)}) collective-permute-start(f32[4,768,1]{1,2,0:T(1,128)S(1)} %get-tuple-element.35), channel_id=1, source_target_pairs={{0,1},{1,2},{2,3},{3,4},{4,5},{5,6},{6,7},{7,8},{8,9},{9,10},{10,1... | collective-permute-start | bytes 36872 | tf_op jit(solution)/shard_map/ppermute | solution.py:26
  233.2 13.8 %copy-start.1 = (f32[4,768,128]{1,2,0:T(8,128)S(1)}, f32[4,768,128]{1,2,0:T(8,128)}, u32[]{:S(2)}) copy-start(f32[4,768,128]{1,2,0:T(8,128)} %copy.23) | copy-start | bytes 4718596
  233.2 13.8 %copy-start.15 = (f32[4,768,128]{2,1,0:T(8,128)S(1)}, f32[4,768,128]{2,1,0:T(8,128)}, u32[]{:S(2)}) copy-start(f32[4,768,128]{2,1,0:T(8,128)} %param.7) | copy-start | bytes 4718596
  233.2 13.8 %copy-start.16 = (f32[4,768,128]{1,2,0:T(8,128)S(1)}, f32[4,768,128]{1,2,0:T(8,128)}, u32[]{:S(2)}) copy-start(f32[4,768,128]{1,2,0:T(8,128)} %copy.19) | copy-start | bytes 4718596
  233.2 13.8 %copy-start.18 = (f32[768]{0:T(1024)S(1)}, f32[768]{0:T(1024)}, u32[]{:S(2)}) copy-start(f32[768]{0:T(1024)} %param.10) | copy-start | bytes 9220
  295.2 24.0 %copy-start.9 = (f32[4,768,128]{1,2,0:T(8,128)}, f32[4,768,128]{1,2,0:T(8,128)S(1)}, u32[]{:S(2)}) copy-start(f32[4,768,128]{1,2,0:T(8,128)S(1)} %broadcast_divide_fusion.3) | copy-start | bytes 4718596
  295.2 11.4 %copy-start.2 = (f32[4,768,128]{1,2,0:T(8,128)S(1)}, f32[4,768,128]{1,2,0:T(8,128)}, u32[]{:S(2)}) copy-start(f32[4,768,128]{1,2,0:T(8,128)} %copy.23) | copy-start | bytes 4718596
  295.3 23.9 %collective-permute-start.4 = (f32[1,768,128]{1,2,0:T(8,128)S(1)}, f32[1,768,128]{1,2,0:T(8,128)S(1)}, u32[]{:S(2)}, u32[]{:S(2)}) collective-permute-start(f32[1,768,128]{1,2,0:T(8,128)S(1)} %get-tuple-element.33), channel_id=1, source_target_pairs={{16,0},{32,16},{48,32},{64,48},{80,64},{96,80},{112,96},{17,1},{33... | collective-permute-start | bytes 1179656 | tf_op jit(solution)/shard_map/ppermute | solution.py:27
  297.5 21.7 %collective-permute-start.5 = (f32[1,768,128]{1,2,0:T(8,128)S(1)}, f32[1,768,128]{1,2,0:T(8,128)S(1)}, u32[]{:S(2)}, u32[]{:S(2)}) collective-permute-start(f32[1,768,128]{1,2,0:T(8,128)S(1)} %get-tuple-element.32), channel_id=1, source_target_pairs={{0,16},{16,32},{32,48},{48,64},{64,80},{80,96},{96,112},{1,17},{17... | collective-permute-start | bytes 1179656 | tf_op jit(solution)/shard_map/ppermute | solution.py:26
  299.9 19.2 %collective-permute-start.6 = (f32[4,768,1]{1,2,0:T(1,128)S(1)}, f32[4,768,1]{1,2,0:T(1,128)S(1)}, u32[]{:S(2)}, u32[]{:S(2)}) collective-permute-start(f32[4,768,1]{1,2,0:T(1,128)S(1)} %get-tuple-element.30), channel_id=1, source_target_pairs={{1,0},{2,1},{3,2},{4,3},{5,4},{6,5},{7,6},{8,7},{9,8},{10,9},{11,1... | collective-permute-start | bytes 36872 | tf_op jit(solution)/shard_map/ppermute | solution.py:27
  304.7 14.5 %collective-permute-start.7 = (f32[4,768,1]{1,2,0:T(1,128)S(1)}, f32[4,768,1]{1,2,0:T(1,128)S(1)}, u32[]{:S(2)}, u32[]{:S(2)}) collective-permute-start(f32[4,768,1]{1,2,0:T(1,128)S(1)} %get-tuple-element.31), channel_id=1, source_target_pairs={{0,1},{1,2},{2,3},{3,4},{4,5},{5,6},{6,7},{7,8},{8,9},{9,10},{10,1... | collective-permute-start | bytes 36872 | tf_op jit(solution)/shard_map/ppermute | solution.py:26
  397.2 23.5 %copy-start.6 = (f32[4,768,128]{1,2,0:T(8,128)}, f32[4,768,128]{1,2,0:T(8,128)S(1)}, u32[]{:S(2)}) copy-start(f32[4,768,128]{1,2,0:T(8,128)S(1)} %broadcast_divide_fusion.2) | copy-start | bytes 4718596
  397.2 10.9 %copy-start.3 = (f32[4,768,128]{1,2,0:T(8,128)S(1)}, f32[4,768,128]{1,2,0:T(8,128)}, u32[]{:S(2)}) copy-start(f32[4,768,128]{1,2,0:T(8,128)} %copy.23) | copy-start | bytes 4718596
  397.3 23.4 %collective-permute-start.8 = (f32[1,768,128]{1,2,0:T(8,128)S(1)}, f32[1,768,128]{1,2,0:T(8,128)S(1)}, u32[]{:S(2)}, u32[]{:S(2)}) collective-permute-start(f32[1,768,128]{1,2,0:T(8,128)S(1)} %get-tuple-element.29), channel_id=1, source_target_pairs={{16,0},{32,16},{48,32},{64,48},{80,64},{96,80},{112,96},{17,1},{33... | collective-permute-start | bytes 1179656 | tf_op jit(solution)/shard_map/ppermute | solution.py:27
  399.5 21.2 %collective-permute-start.9 = (f32[1,768,128]{1,2,0:T(8,128)S(1)}, f32[1,768,128]{1,2,0:T(8,128)S(1)}, u32[]{:S(2)}, u32[]{:S(2)}) collective-permute-start(f32[1,768,128]{1,2,0:T(8,128)S(1)} %get-tuple-element.28), channel_id=1, source_target_pairs={{0,16},{16,32},{32,48},{48,64},{64,80},{80,96},{96,112},{1,17},{17... | collective-permute-start | bytes 1179656 | tf_op jit(solution)/shard_map/ppermute | solution.py:26
  401.9 18.7 %collective-permute-start.10 = (f32[4,768,1]{1,2,0:T(1,128)S(1)}, f32[4,768,1]{1,2,0:T(1,128)S(1)}, u32[]{:S(2)}, u32[]{:S(2)}) collective-permute-start(f32[4,768,1]{1,2,0:T(1,128)S(1)} %get-tuple-element.26), channel_id=1, source_target_pairs={{1,0},{2,1},{3,2},{4,3},{5,4},{6,5},{7,6},{8,7},{9,8},{10,9},{11,1... | collective-permute-start | bytes 36872 | tf_op jit(solution)/shard_map/ppermute | solution.py:27
  404.0 16.7 %copy-start.10 = (f32[4,768,128]{1,2,0:T(8,128)S(1)}, f32[4,768,128]{1,2,0:T(8,128)}, u32[]{:S(2)}) copy-start(f32[4,768,128]{1,2,0:T(8,128)} %copy-done.9) | copy-start | bytes 4718596
  404.0 16.7 %collective-permute-start.11 = (f32[4,768,1]{1,2,0:T(1,128)S(1)}, f32[4,768,1]{1,2,0:T(1,128)S(1)}, u32[]{:S(2)}, u32[]{:S(2)}) collective-permute-start(f32[4,768,1]{1,2,0:T(1,128)S(1)} %get-tuple-element.27), channel_id=1, source_target_pairs={{0,1},{1,2},{2,3},{3,4},{4,5},{5,6},{6,7},{7,8},{8,9},{9,10},{10,1... | collective-permute-start | bytes 36872 | tf_op jit(solution)/shard_map/ppermute | solution.py:26
  499.3 23.7 %copy-start.13 = (f32[4,768,128]{1,2,0:T(8,128)}, f32[4,768,128]{1,2,0:T(8,128)S(1)}, u32[]{:S(2)}) copy-start(f32[4,768,128]{1,2,0:T(8,128)S(1)} %broadcast_divide_fusion.1) | copy-start | bytes 4718596
  499.3 11.1 %copy-start.4 = (f32[4,768,128]{1,2,0:T(8,128)S(1)}, f32[4,768,128]{1,2,0:T(8,128)}, u32[]{:S(2)}) copy-start(f32[4,768,128]{1,2,0:T(8,128)} %copy.23) | copy-start | bytes 4718596
  499.4 23.6 %collective-permute-start.12 = (f32[1,768,128]{1,2,0:T(8,128)S(1)}, f32[1,768,128]{1,2,0:T(8,128)S(1)}, u32[]{:S(2)}, u32[]{:S(2)}) collective-permute-start(f32[1,768,128]{1,2,0:T(8,128)S(1)} %get-tuple-element.25), channel_id=1, source_target_pairs={{16,0},{32,16},{48,32},{64,48},{80,64},{96,80},{112,96},{17,1},{33... | collective-permute-start | bytes 1179656 | tf_op jit(solution)/shard_map/ppermute | solution.py:27
  501.6 21.4 %collective-permute-start.13 = (f32[1,768,128]{1,2,0:T(8,128)S(1)}, f32[1,768,128]{1,2,0:T(8,128)S(1)}, u32[]{:S(2)}, u32[]{:S(2)}) collective-permute-start(f32[1,768,128]{1,2,0:T(8,128)S(1)} %get-tuple-element.24), channel_id=1, source_target_pairs={{0,16},{16,32},{32,48},{48,64},{64,80},{80,96},{96,112},{1,17},{17... | collective-permute-start | bytes 1179656 | tf_op jit(solution)/shard_map/ppermute | solution.py:26
  504.0 18.9 %collective-permute-start.14 = (f32[4,768,1]{1,2,0:T(1,128)S(1)}, f32[4,768,1]{1,2,0:T(1,128)S(1)}, u32[]{:S(2)}, u32[]{:S(2)}) collective-permute-start(f32[4,768,1]{1,2,0:T(1,128)S(1)} %get-tuple-element.22), channel_id=1, source_target_pairs={{1,0},{2,1},{3,2},{4,3},{5,4},{6,5},{7,6},{8,7},{9,8},{10,9},{11,1... | collective-permute-start | bytes 36872 | tf_op jit(solution)/shard_map/ppermute | solution.py:27
  505.9 17.0 %copy-start.7 = (f32[4,768,128]{1,2,0:T(8,128)S(1)}, f32[4,768,128]{1,2,0:T(8,128)}, u32[]{:S(2)}) copy-start(f32[4,768,128]{1,2,0:T(8,128)} %copy-done.6) | copy-start | bytes 4718596
  506.0 17.0 %copy-start.11 = (f32[4,768,128]{1,2,0:T(8,128)S(1)}, f32[4,768,128]{1,2,0:T(8,128)}, u32[]{:S(2)}) copy-start(f32[4,768,128]{1,2,0:T(8,128)} %copy-done.9) | copy-start | bytes 4718596
  506.0 17.0 %collective-permute-start.15 = (f32[4,768,1]{1,2,0:T(1,128)S(1)}, f32[4,768,1]{1,2,0:T(1,128)S(1)}, u32[]{:S(2)}, u32[]{:S(2)}) collective-permute-start(f32[4,768,1]{1,2,0:T(1,128)S(1)} %get-tuple-element.23), channel_id=1, source_target_pairs={{0,1},{1,2},{2,3},{3,4},{4,5},{5,6},{6,7},{7,8},{8,9},{9,10},{10,1... | collective-permute-start | bytes 36872 | tf_op jit(solution)/shard_map/ppermute | solution.py:26
  603.9 11.0 %copy-start.5 = (f32[4,768,128]{1,2,0:T(8,128)S(1)}, f32[4,768,128]{1,2,0:T(8,128)}, u32[]{:S(2)}) copy-start(f32[4,768,128]{1,2,0:T(8,128)} %copy.23) | copy-start | bytes 4718596
  604.0 23.5 %collective-permute-start.16 = (f32[1,768,128]{1,2,0:T(8,128)S(1)}, f32[1,768,128]{1,2,0:T(8,128)S(1)}, u32[]{:S(2)}, u32[]{:S(2)}) collective-permute-start(f32[1,768,128]{1,2,0:T(8,128)S(1)} %get-tuple-element.21), channel_id=1, source_target_pairs={{16,0},{32,16},{48,32},{64,48},{80,64},{96,80},{112,96},{17,1},{33... | collective-permute-start | bytes 1179656 | tf_op jit(solution)/shard_map/ppermute | solution.py:27
  606.1 21.4 %collective-permute-start.17 = (f32[1,768,128]{1,2,0:T(8,128)S(1)}, f32[1,768,128]{1,2,0:T(8,128)S(1)}, u32[]{:S(2)}, u32[]{:S(2)}) collective-permute-start(f32[1,768,128]{1,2,0:T(8,128)S(1)} %get-tuple-element.20), channel_id=1, source_target_pairs={{0,16},{16,32},{32,48},{48,64},{64,80},{80,96},{96,112},{1,17},{17... | collective-permute-start | bytes 1179656 | tf_op jit(solution)/shard_map/ppermute | solution.py:26
  608.5 19.0 %collective-permute-start.18 = (f32[4,768,1]{1,2,0:T(1,128)S(1)}, f32[4,768,1]{1,2,0:T(1,128)S(1)}, u32[]{:S(2)}, u32[]{:S(2)}) collective-permute-start(f32[4,768,1]{1,2,0:T(1,128)S(1)} %get-tuple-element.18), channel_id=1, source_target_pairs={{1,0},{2,1},{3,2},{4,3},{5,4},{6,5},{7,6},{8,7},{9,8},{10,9},{11,1... | collective-permute-start | bytes 36872 | tf_op jit(solution)/shard_map/ppermute | solution.py:27
  610.4 17.1 %copy-start.8 = (f32[4,768,128]{1,2,0:T(8,128)S(1)}, f32[4,768,128]{1,2,0:T(8,128)}, u32[]{:S(2)}) copy-start(f32[4,768,128]{1,2,0:T(8,128)} %copy-done.6) | copy-start | bytes 4718596
  610.4 17.1 %copy-start.12 = (f32[4,768,128]{1,2,0:T(8,128)S(1)}, f32[4,768,128]{1,2,0:T(8,128)}, u32[]{:S(2)}) copy-start(f32[4,768,128]{1,2,0:T(8,128)} %copy-done.9) | copy-start | bytes 4718596
  610.5 17.1 %copy-start.14 = (f32[4,768,128]{1,2,0:T(8,128)S(1)}, f32[4,768,128]{1,2,0:T(8,128)}, u32[]{:S(2)}) copy-start(f32[4,768,128]{1,2,0:T(8,128)} %copy-done.13) | copy-start | bytes 4718596
  610.5 17.0 %collective-permute-start.19 = (f32[4,768,1]{1,2,0:T(1,128)S(1)}, f32[4,768,1]{1,2,0:T(1,128)S(1)}, u32[]{:S(2)}, u32[]{:S(2)}) collective-permute-start(f32[4,768,1]{1,2,0:T(1,128)S(1)} %get-tuple-element.19), channel_id=1, source_target_pairs={{0,1},{1,2},{2,3},{3,4},{4,5},{5,6},{6,7},{7,8},{8,9},{9,10},{10,1... | collective-permute-start | bytes 36872 | tf_op jit(solution)/shard_map/ppermute | solution.py:26
